TPU v7x, 32 devices: a whole 2x2x4 slice. The times are simulated.
32 devices in a mesh: mod: 2 (over y), exp: 16 (over z, x, core).
Axes of the slice: x: 2, y: 2, z: 4, core: 2. Of those that a mesh axis runs over, the one named last changes fastest.
Arguments:
- tokens: bfloat16 [2, 8192, 1024], P('mod', 'exp'), may hold values from -60 to 60
- bottleneck: bfloat16 [64, 4, 1024], P('exp'), may hold values from -6 to 6
- clip_ids: int32 [2, 8192], P('mod', 'exp'), may hold values from 0 to 63, as said below
- expert_ids: int32 [2, 8192], P('mod', 'exp'), may hold values from 0 to 15, as said below
- slots: int32 [2, 8192], P('mod', 'exp'), may hold values from 0 to 127, as said below
- norm1_gain: bfloat16 [2, 1024], P('mod'), may hold values from 0.099609375 to 1.8984375
- attn_qkv: bfloat16 [2, 1024, 3072], P('mod'), may hold values from -2 to 2
- attn_out: bfloat16 [2, 1024, 1024], P('mod'), may hold values from -0.1875 to 0.1875
- norm2_gain: bfloat16 [2, 1024], P('mod'), may hold values from 0.099609375 to 1.8984375
- router: bfloat16 [1024, 16], replicated, may hold values from -0.1875 to 0.1875
- fc_in: bfloat16 [16, 1024, 4096], P('exp'), may hold values from -0.1875 to 0.1875
- fc_out: bfloat16 [16, 4096, 1024], P('exp'), may hold values from -0.09375 to 0.09375
Outputs:
- mixed_tokens: bfloat16 [2, 8192, 1024], P('mod', 'exp')
- new_bottleneck: bfloat16 [64, 4, 1024], P('exp')
Inputs may be any that keep to these rules, and one draw needn't show every extreme that they name: `clip_ids`: Non-decreasing in each modality; the tokens of block b of 512 rows belong to clips b * 4 to (b + 1) * 4 - 1, each of which has one or more of them. `expert_ids`: each token's single expert. For the k tokens of one block of 512 rows of one modality that share an expert, the slots are 0 to k - 1 in some order; k is at most 128; in every block of each modality one expert, the same for all blocks of that modality, has k = 128.
All inputs are finite; a program needn't handle non-finite values.
Results may differ from a plain program's by a relative error of at most 0.0085.
Values may be sent and summed in bfloat16 or wider, within the bound.
A program may use at most 128 MiB of HBM per device.

v0:
```python
import math

import jax
import jax.numpy as jnp
from jax import lax
from jax.sharding import PartitionSpec as P

HEAD = 64
CAP_FACTOR = 2


EPSILON = 1e-06


def layer_norm(features, scales):
    row_mean = jnp.mean(features, axis=-1, keepdims=True)
    centred = features - row_mean
    spread = jnp.mean(centred * centred, axis=-1, keepdims=True)
    return centred * lax.rsqrt(spread + EPSILON) * scales.astype(jnp.float32)


def attend(token_rows, latent_rows, token_clip, clip_start, scales, w_qkv, w_out):
    n_clips, n_latent, model_width = latent_rows.shape
    n_tokens = token_rows.shape[0]
    all_rows = jnp.concatenate(
        [token_rows, latent_rows.reshape(n_clips * n_latent, model_width)], axis=0
    )
    row_count = all_rows.shape[0]
    head_count = model_width // HEAD
    normed = layer_norm(all_rows.astype(jnp.float32), scales).astype(jnp.bfloat16)
    packed = jnp.dot(normed, w_qkv, preferred_element_type=jnp.float32).astype(jnp.bfloat16)
    queries = packed[:, :model_width].reshape(row_count, head_count, HEAD)
    key_rows = packed[:, model_width : 2 * model_width].reshape(row_count, head_count, HEAD)
    value_rows = packed[:, 2 * model_width :].reshape(row_count, head_count, HEAD)
    latent_clip = clip_start + jnp.arange(n_clips * n_latent, dtype=jnp.int32) // n_latent
    row_clip = jnp.concatenate([token_clip, latent_clip])
    allowed = row_clip[:, None] == row_clip[None, :]
    scores = jnp.einsum("qhd,khd->hqk", queries, key_rows, preferred_element_type=jnp.float32) * (
        1.0 / math.sqrt(HEAD)
    )
    scores = jnp.where(allowed[None, :, :], scores, -jnp.inf)
    row_max = jnp.max(scores, axis=-1, keepdims=True)
    weights = jnp.exp(scores - row_max)
    attn_weights = (weights / jnp.sum(weights, axis=-1, keepdims=True)).astype(jnp.bfloat16)
    attended = jnp.einsum(
        "hqk,khd->qhd", attn_weights, value_rows, preferred_element_type=jnp.float32
    )
    attended = attended.reshape(row_count, model_width).astype(jnp.bfloat16)
    updated = all_rows.astype(jnp.float32) + jnp.dot(
        attended, w_out, preferred_element_type=jnp.float32
    )
    return (updated[:n_tokens], updated[n_tokens:].reshape(n_clips, n_latent, model_width))


def apply_experts(received, weight_in, weight_out):
    local_count = weight_in.shape[0]
    row_count, slot_count, model_width = received.shape
    grouped = received.reshape(row_count // local_count, local_count, slot_count, model_width)
    hidden_units = jnp.einsum(
        "secd,edf->secf", grouped, weight_in, preferred_element_type=jnp.float32
    )
    activated = jax.nn.gelu(hidden_units, approximate=False).astype(jnp.bfloat16)
    outputs = jnp.einsum(
        "secf,efd->secd", activated, weight_out, preferred_element_type=jnp.float32
    )
    return outputs.astype(jnp.bfloat16).reshape(row_count, slot_count, model_width)


def mixture(mid_tokens, chosen, slot_ids, scales, router, fc_in, fc_out):
    model_width = mid_tokens.shape[1]
    expert_count = router.shape[1]
    capacity = CAP_FACTOR * mid_tokens.shape[0] // expert_count
    slot_total = expert_count * capacity
    expert_in = layer_norm(mid_tokens, scales).astype(jnp.bfloat16)
    logits = jnp.dot(expert_in, router, preferred_element_type=jnp.float32)
    column = jnp.arange(expert_count, dtype=jnp.int32)
    picked = jnp.sum(
        jnp.where(column[None, :] == chosen[:, None], logits, jnp.zeros_like(logits)), axis=1
    )
    gate_value = jax.nn.sigmoid(picked)
    served = slot_ids < capacity
    position = jnp.where(served, chosen * capacity + slot_ids, slot_total)
    buffer = (
        jnp.zeros((slot_total, model_width), jnp.bfloat16).at[position].set(expert_in, mode="drop")
    )
    buffer = buffer.reshape(expert_count, capacity, model_width)
    results = lax.all_to_all(
        apply_experts(
            lax.all_to_all(buffer, "exp", split_axis=0, concat_axis=0, tiled=True), fc_in, fc_out
        ),
        "exp",
        split_axis=0,
        concat_axis=0,
        tiled=True,
    )
    returned = jnp.take(
        results.reshape(slot_total, model_width), position, axis=0, mode="fill", fill_value=0
    )
    return (mid_tokens + gate_value[:, None] * returned.astype(jnp.float32)).astype(jnp.bfloat16)


def average_latent(mid_latent):
    summed = lax.psum(mid_latent.astype(jnp.bfloat16), "mod").astype(jnp.float32)
    return (summed * 0.5).astype(jnp.bfloat16)


def on_device(
    tokens,
    bottleneck,
    clip_ids,
    expert_ids,
    slots,
    norm1_gain,
    attn_qkv,
    attn_out,
    norm2_gain,
    router,
    fc_in,
    fc_out,
):
    clip_start = lax.axis_index("exp") * bottleneck.shape[0]
    mid_tokens, mid_latent = attend(
        tokens[0], bottleneck, clip_ids[0], clip_start, norm1_gain[0], attn_qkv[0], attn_out[0]
    )
    new_bottleneck = average_latent(mid_latent)
    mixed_tokens = mixture(
        mid_tokens, expert_ids[0], slots[0], norm2_gain[0], router, fc_in, fc_out
    )
    return (mixed_tokens[None], new_bottleneck)


def solution(mesh):
    in_specs = (
        P("mod", "exp", None),
        P("exp", None, None),
        P("mod", "exp"),
        P("mod", "exp"),
        P("mod", "exp"),
        P("mod", None),
        P("mod", None, None),
        P("mod", None, None),
        P("mod", None),
        P(),
        P("exp", None, None),
        P("exp", None, None),
    )
    out_specs = (P("mod", "exp", None), P("exp", None, None))
    return jax.shard_map(
        on_device, mesh=mesh, in_specs=in_specs, out_specs=out_specs, check_vma=False
    )
```

profile of v0, /device:TPU:29, one launch (start us, length us, event | category | flops | bytes accessed | tf_op | source)
XLA Modules:
  0.0 218.5 jit_solution(17665730656248300949)
XLA Ops:
  0.7 0.9 reshape.163
  1.6 1.5 convert_reduce_fusion
  3.0 1.7 fusion.35
  5.4 6.7 %fusion.30 = bf16[528,3072]{1,0:T(8,128)(2,1)S(1)} fusion(bf16[1,1024,3072]{2,1,0:T(8,128)(2,1)} %param.18, f32[1024]{0:T(1024)S(1)} %bitcast.160, f32[528]{0:T(1024)S(1)} %add_rsqrt_fusion, f32[528]{0:T(1024)S(1)} %broadcast_multiply_fusion, bf16[16,1024]{1,0:T(8,128)(2,1)S(1)} %reshape.163, bf16[512,1024]{1,0:T(8,128)(2,1)} %bitcast.148), kind=kOutput, calls=%fused_computation.40 | convolution fusion | flops 3327836160 | bytes 10625152 | tf_op jit(solution)/shard_map/dot_general | solution.py:31
  12.2 1.7 fusion.96
  13.8 2.4 %copy.19 = bf16[528,1024]{0,1:T(8,128)(2,1)} copy(bf16[528,1024]{1,0:T(8,128)(2,1)} %get-tuple-element.3) | data formatting | bytes 2162688 | tf_op jit(solution)/shard_map/slice | solution.py:32
  16.2 2.4 %copy.20 = bf16[528,1024]{0,1:T(8,128)(2,1)} copy(bf16[528,1024]{1,0:T(8,128)(2,1)} %get-tuple-element.2) | data formatting | bytes 2162688 | tf_op jit(solution)/shard_map/slice | solution.py:33
  18.6 1.0 broadcast_compare_fusion
  19.6 1.5 copy.18
  21.1 12.8 %fusion.97 = (f32[16,528]{1,0:T(8,128)S(1)}, f32[16,528,528]{1,2,0:T(8,128)}) fusion(pred[528,528]{0,1:T(8,128)(4,1)} %broadcast_compare_fusion, bf16[528,16,64]{0,2,1:T(8,128)(2,1)} %bitcast.150, bf16[528,16,64]{0,2,1:T(8,128)(2,1)} %bitcast.151), kind=kOutput, calls=%fused_computation.121 | convolution fusion | flops 588792320 | bytes 20317440 | tf_op jit(solution)/shard_map/sub | solution.py:43
  33.9 9.4 %fusion.49 = bf16[16,64,528]{2,1,0:T(8,128)(2,1)S(1)} fusion(bf16[528,16,64]{0,2,1:T(8,128)(2,1)S(1)} %bitcast.152, f32[16,528,528]{1,2,0:T(8,128)} %get-tuple-element.6, f32[16,528]{1,0:T(8,128)S(1)} %get-tuple-element.5), kind=kOutput, calls=%fused_computation.56 | convolution fusion | flops 580411392 | bytes 20038656 | tf_op jit(solution)/shard_map/hqk,khd->qhd/dot_general | solution.py:45
  43.4 1.4 convert_add_fusion
  44.9 1.2 copy-done.2
  46.5 4.4 %scatter_custom_fusion = bf16[1024,1024]{1,0:T(8,128)(2,1)S(1)} fusion(s32[512]{0:T(512)S(1)} %bitcast.155, bf16[]{:T(256)} %constant.26.clone.1, f32[528,1024]{1,0:T(8,128)} %copy-done.2, f32[1024]{0:T(1024)S(1)} %bitcast.153, f32[512]{0:T(512)S(1)} %add_rsqrt_fusion.1, f32[512]{0:T(512)S(1)} %broadcast_multiply_fusion.1), kind=kCustom, calls=%fused_computation.65 | custom fusion | flops 2097152 | bytes 4203008 | tf_op jit(solution)/shard_map/scatter | solution.py:84
  50.9 52.4 %all_to_all.10 = bf16[16,64,1024]{2,1,0:T(8,128)(2,1)S(1)} all-to-all(bf16[16,64,1024]{2,1,0:T(8,128)(2,1)S(1)} %bitcast.145), channel_id=1, replica_groups=mesh['mod'=2,'exp'=16] {'exp'}, dimensions={0} | all-to-all | bytes 4194304 | tf_op jit(solution)/shard_map/all_to_all | solution.py:89
  103.4 44.9 %fusion.116 = bf16[16,64,4096]{2,1,0:T(8,128)(2,1)S(1)} fusion(bf16[16,64,1024]{2,1,0:T(8,128)(2,1)S(1)} %all_to_all.10, bf16[1,1024,4096]{2,1,0:T(8,128)(2,1)} %param.22), kind=kOutput, calls=%fused_computation.33.clone.clone.clone.1 | convolution fusion | flops 8862564352 | bytes 18874368 | tf_op jit(solution)/shard_map/secd,edf->secf/dot_general | solution.py:59
  148.3 12.2 %fusion.40 = bf16[16,64,1024]{2,1,0:T(8,128)(2,1)} fusion(bf16[1,4096,1024]{2,1,0:T(8,128)(2,1)} %param.23, bf16[16,64,4096]{2,1,0:T(8,128)(2,1)S(1)} %fusion.116), kind=kOutput, calls=%fused_computation.54 | convolution fusion | flops 8590983168 | bytes 18874368 | tf_op jit(solution)/shard_map/secf,efd->secd/dot_general | solution.py:63
  160.5 6.0 %all-to-all-start.1 = ((bf16[16,64,1024]{2,1,0:T(8,128)(2,1)}), bf16[16,64,1024]{2,1,0:T(8,128)(2,1)}, u32[]{:S(2)}, u32[]{:S(2)}) async-start(bf16[16,64,1024]{2,1,0:T(8,128)(2,1)} %fusion.40), calls=%async_computation.1 | async-start | bytes 4194304 | tf_op jit(solution)/shard_map/all_to_all | solution.py:87
  166.5 0.8 slice.35
  167.4 6.1 %psum.7 = bf16[4,4,1024]{2,1,0:T(4,128)(2,1)S(1)} all-reduce(bf16[4,4,1024]{2,1,0:T(4,128)(2,1)S(1)} %convert_element_type.66), channel_id=1, replica_groups=mesh['mod'=2,'exp'=16] {'mod'}, use_global_device_ids=true, to_apply=%region_8.9 | all-reduce | flops 16384 | bytes 65536 | tf_op jit(solution)/shard_map/psum | solution.py:103
  173.5 2.1 fusion.54
  176.3 34.5 %all-to-all-done.1 = bf16[16,64,1024]{2,1,0:T(8,128)(2,1)} async-done(((bf16[16,64,1024]{2,1,0:T(8,128)(2,1)}), bf16[16,64,1024]{2,1,0:T(8,128)(2,1)}, u32[]{:S(2)}, u32[]{:S(2)}) %all-to-all-start.1) | async-done | bytes 2097184 | tf_op jit(solution)/shard_map/all_to_all | solution.py:87
  210.8 4.7 %gather_fusion = bf16[512,1024]{1,0:T(8,128)(2,1)S(1)} fusion(bf16[1024,1024]{1,0:T(8,128)(2,1)} %bitcast.29, s32[1024]{0:T(1024)S(1)} %pad_clamp_fusion), kind=kCustom, calls=%fused_computation | custom fusion | bytes 2099200 | tf_op jit(solution)/shard_map/jit(_take)/gather | solution.py:96
  215.6 2.9 %fusion.59 = bf16[1,512,1024]{2,1,0:T(8,128)(2,1)} fusion(f32[528,1024]{1,0:T(8,128)} %copy-done.2, bf16[512,1024]{1,0:T(8,128)(2,1)S(1)} %gather_fusion, f32[512]{0:T(512)S(1)} %add_divide_fusion, pred[512]{0:T(512)(128)(4,1)S(1)} %compare_and_fusion), kind=kLoop, calls=%fused_computation.64 | loop fusion | flops 2621440 | bytes 4196864 | tf_op jit(solution)/shard_map/broadcast_in_dim | solution.py:129
  (35 shorter events, 2.0 us)
Async XLA Ops:
  0.6 42.7 %copy-start = (bf16[1,1024,1024]{2,1,0:T(8,128)(2,1)S(1)}, bf16[1,1024,1024]{2,1,0:T(8,128)(2,1)}, u32[]{:S(2)}) copy-start(bf16[1,1024,1024]{2,1,0:T(8,128)(2,1)} %param.19) | copy-start | bytes 6291460
  12.1 6.5 %copy-start.8 = (s32[1,512]{1,0:T(1,128)S(1)}, s32[1,512]{1,0:T(1,128)}, u32[]{:S(2)}) copy-start(s32[1,512]{1,0:T(1,128)} %param.14) | copy-start | bytes 6148
  21.1 12.8 %copy-start.4 = (bf16[528,1024]{0,1:T(8,128)(2,1)S(1)}, bf16[528,1024]{0,1:T(8,128)(2,1)}, u32[]{:S(2)}) copy-start(bf16[528,1024]{0,1:T(8,128)(2,1)} %copy.18) | copy-start | bytes 3244036
  33.9 9.4 %copy-start.3 = (bf16[1,512,1024]{2,1,0:T(8,128)(2,1)S(1)}, bf16[1,512,1024]{2,1,0:T(8,128)(2,1)}, u32[]{:S(2)}) copy-start(bf16[1,512,1024]{2,1,0:T(8,128)(2,1)} %param.12) | copy-start | bytes 3145732
  43.3 3.1 %copy-start.7 = (bf16[1,1024]{1,0:T(2,128)(2,1)S(1)}, bf16[1,1024]{1,0:T(2,128)(2,1)}, u32[]{:S(2)}) copy-start(bf16[1,1024]{1,0:T(2,128)(2,1)} %param.20) | copy-start | bytes 6148
  43.3 3.1 %copy-start.5 = (s32[1,512]{1,0:T(1,128)S(1)}, s32[1,512]{1,0:T(1,128)}, u32[]{:S(2)}) copy-start(s32[1,512]{1,0:T(1,128)} %param.16) | copy-start | bytes 6148
  43.4 3.1 %copy-start.6 = (s32[1,512]{1,0:T(1,128)S(1)}, s32[1,512]{1,0:T(1,128)}, u32[]{:S(2)}) copy-start(s32[1,512]{1,0:T(1,128)} %param.15) | copy-start | bytes 6148
  44.7 1.4 copy-start.2
  148.2 25.3 %copy-start.9 = (bf16[1024,16]{0,1:T(8,128)(2,1)S(1)}, bf16[1024,16]{0,1:T(8,128)(2,1)}, u32[]{:S(2)}) copy-start(bf16[1024,16]{0,1:T(8,128)(2,1)} %param.21) | copy-start | bytes 98308
  160.5 50.3 %all-to-all-start.1 = ((bf16[16,64,1024]{2,1,0:T(8,128)(2,1)}), bf16[16,64,1024]{2,1,0:T(8,128)(2,1)}, u32[]{:S(2)}, u32[]{:S(2)}) async-start(bf16[16,64,1024]{2,1,0:T(8,128)(2,1)} %fusion.40), calls=%async_computation.1 | async-start | bytes 4194304 | tf_op jit(solution)/shard_map/all_to_all | solution.py:87
  210.8 7.7 %copy-start.1 = (bf16[1,1024,1024]{2,1,0:T(8,128)(2,1)S(1)}, bf16[1,1024,1024]{2,1,0:T(8,128)(2,1)}, u32[]{:S(2)}) copy-start(bf16[1,1024,1024]{2,1,0:T(8,128)(2,1)} %param.19) | copy-start | bytes 6291460
where the time goes:
time: 222 us; the launch traced here: 219 us
  matrix products  89.5 us (40%)
  blocking collectives  58.6 us (26%)
  waiting for transfers between devices  34.5 us (16%)
  local copies, waits for them, and re-layouts  15.7 us (7%)
  other arithmetic  13.4 us (6%)
  starting transfers between devices  5.99 us (3%)
    all_to_all x1, blocking collectives, mixture(): lax.all_to_all(buffer, 'exp', split_axis=0, concat_axis=0, tiled=True)  52.4 us
    dot_general x1, matrix products, apply_experts(): jnp.einsum('secd,edf->secf', grouped, weight_in, preferred_element_type=j...  44.9 us
    all_to_all x1, waiting for transfers between devices, mixture(): lax.all_to_all(apply_experts(lax.all_to_all(buffer, 'exp', split_axis=0,...  34.5 us
    sub x1, matrix products, attend(): weights = jnp.exp(scores - row_max)  12.8 us
    dot_general x1, matrix products, apply_experts(): jnp.einsum('secf,efd->secd', activated, weight_out, preferred_element_typ...  12.2 us
    dot_general x1, matrix products, attend(): jnp.einsum('hqk,khd->qhd', attn_weights, value_rows, preferred_element_ty...  9.41 us
    dot_general x1, matrix products, attend(): jnp.dot(normed, w_qkv, preferred_element_type=jnp.float32)  6.74 us
    psum x1, blocking collectives, average_latent(): lax.psum(mid_latent.astype(jnp.bfloat16), 'mod').astype(jnp.float32)  6.14 us
  transfers between devices with their start and end apart: 1, of which 1 were waited for; matrix products, arithmetic and copies ran while one was open for 2% of the time, Pallas kernels for 0%

commit v1 on v0

--- a/solution.py
+++ b/solution.py
@@ -1,10 +1,14 @@
+import functools
 import math
 
 import jax
 import jax.numpy as jnp
 from jax import lax
+from jax.experimental import pallas as pl
+from jax.experimental.pallas import tpu as pltpu
 from jax.sharding import PartitionSpec as P
 
+MESH = pl.DeviceIdType.MESH
 HEAD = 64
 CAP_FACTOR = 2
 
@@ -52,21 +56,196 @@
     return (updated[:n_tokens], updated[n_tokens:].reshape(n_clips, n_latent, model_width))
 
 
-def apply_experts(received, weight_in, weight_out):
-    local_count = weight_in.shape[0]
-    row_count, slot_count, model_width = received.shape
-    grouped = received.reshape(row_count // local_count, local_count, slot_count, model_width)
-    hidden_units = jnp.einsum(
-        "secd,edf->secf", grouped, weight_in, preferred_element_type=jnp.float32
-    )
-    activated = jax.nn.gelu(hidden_units, approximate=False).astype(jnp.bfloat16)
-    outputs = jnp.einsum(
-        "secf,efd->secd", activated, weight_out, preferred_element_type=jnp.float32
-    )
-    return outputs.astype(jnp.bfloat16).reshape(row_count, slot_count, model_width)
-
-
-def mixture(mid_tokens, chosen, slot_ids, scales, router, fc_in, fc_out):
+def gelu(x):
+    half = 0.5 * x
+    return half + half * lax.erf(x * (1.0 / math.sqrt(2.0)))
+
+
+def near_count(size):
+    return 4 if size % 4 == 0 else 1
+
+
+def moe_kernel(
+    size,
+    cap,
+    tile,
+    latent_ref,
+    buf_ref,
+    w_in_hbm,
+    w_out_hbm,
+    out_ref,
+    mean_ref,
+    w_in,
+    w_out,
+    recv,
+    res,
+    acc,
+    act,
+    peer_latent,
+    w_sems,
+    own_sems,
+    lat_sems,
+    send_sems,
+    recv_sems,
+    back_send,
+    back_recv,
+):
+    near = near_count(size)
+    far = size // near
+    me = lax.axis_index("exp")
+    mod = lax.axis_index("mod")
+    high, low = me // near, me % near
+    shifts = [0] + sorted(range(1, far), key=lambda s: (abs(2 * s - far), s))
+    order = [(s, d) for s in shifts for d in range(near)]
+
+    def ahead(step):
+        s, d = order[step]
+        return ((high + s) % far) * near + (low + d) % near
+
+    def behind(step):
+        s, d = order[step]
+        return ((high + far - s) % far) * near + (low + near - d) % near
+
+    def block(index):
+        return pl.ds(pl.multiple_of(index * cap, cap), cap)
+
+    load_in = pltpu.make_async_copy(w_in_hbm, w_in, w_sems.at[0])
+    load_out = pltpu.make_async_copy(w_out_hbm, w_out, w_sems.at[1])
+    load_in.start()
+    load_out.start()
+
+    barrier = pltpu.get_barrier_semaphore()
+    for step in range(1, size):
+        pl.semaphore_signal(barrier, inc=1, device_id=(mod, ahead(step)), device_id_type=MESH)
+    pl.semaphore_signal(barrier, inc=1, device_id=(1 - mod, me), device_id_type=MESH)
+    pl.semaphore_wait(barrier, size)
+
+    sends = [None]
+    for step in range(1, size):
+        sends.append(
+            pltpu.make_async_remote_copy(
+                src_ref=buf_ref.at[block(ahead(step))],
+                dst_ref=recv.at[pl.ds(step * cap, cap)],
+                send_sem=send_sems.at[step],
+                recv_sem=recv_sems.at[step],
+                device_id=(mod, ahead(step)),
+                device_id_type=MESH,
+            )
+        )
+    backs = [None]
+    for step in range(1, size):
+        backs.append(
+            pltpu.make_async_remote_copy(
+                src_ref=res.at[pl.ds(step * cap, cap)],
+                dst_ref=out_ref.at[block(me)],
+                send_sem=back_send.at[step],
+                recv_sem=back_recv.at[step],
+                device_id=(mod, behind(step)),
+                device_id_type=MESH,
+            )
+        )
+    for step in range(1, size):
+        sends[step].start()
+    latent_copy = pltpu.make_async_remote_copy(
+        src_ref=latent_ref,
+        dst_ref=peer_latent,
+        send_sem=lat_sems.at[0],
+        recv_sem=lat_sems.at[1],
+        device_id=(1 - mod, me),
+        device_id_type=MESH,
+    )
+    latent_copy.start()
+    own = pltpu.make_async_copy(buf_ref.at[block(me)], recv.at[pl.ds(0, cap)], own_sems.at[0])
+    own.start()
+    own.wait()
+
+    groups = 4 if size % 4 == 0 else 1
+    per = size // groups
+    rows = per * cap
+    tiles = w_in.shape[1] // tile
+    own_back = pltpu.make_async_copy(res.at[pl.ds(0, cap)], out_ref.at[block(me)], own_sems.at[1])
+    for g in range(groups):
+        for step in range(g * per, (g + 1) * per):
+            if step:
+                sends[step].wait_recv()
+        if g == 0:
+            load_in.wait()
+            load_out.wait()
+        here = pl.ds(g * rows, rows)
+
+        def hidden(t):
+            cols = pl.ds(pl.multiple_of(t * tile, tile), tile)
+            return gelu(
+                jnp.dot(recv[here, :], w_in[:, cols], preferred_element_type=jnp.float32)
+            ).astype(jnp.bfloat16)
+
+        def project(t, slot):
+            cols = pl.ds(pl.multiple_of(t * tile, tile), tile)
+            return jnp.dot(act[slot], w_out[cols, :], preferred_element_type=jnp.float32)
+
+        act[0] = hidden(0)
+        acc[...] = jnp.zeros_like(acc)
+
+        def body(t, carry):
+            acc[...] += project(t - 1, (t + 1) % 2)
+            act[t % 2] = hidden(t)
+            return carry
+
+        lax.fori_loop(1, tiles, body, 0)
+        res[here, :] = (acc[...] + project(tiles - 1, (tiles - 1) % 2)).astype(jnp.bfloat16)
+        for step in range(g * per, (g + 1) * per):
+            if step:
+                backs[step].start()
+            else:
+                own_back.start()
+
+    latent_copy.wait()
+    mean_ref[...] = ((latent_ref[...] + peer_latent[...]) * 0.5).astype(jnp.bfloat16)
+    own_back.wait()
+    for step in range(1, size):
+        sends[step].wait_send()
+        backs[step].wait()
+
+
+def exchange_experts(mid_latent, buffer, weight_in, weight_out, size):
+    rows, width = buffer.shape
+    cap = rows // size
+    hidden_width = weight_in.shape[1]
+    tile = 512
+    groups = 4 if size % 4 == 0 else 1
+    vmem = pl.BlockSpec(memory_space=pltpu.VMEM)
+    hbm = pl.BlockSpec(memory_space=pl.ANY)
+    return pl.pallas_call(
+        functools.partial(moe_kernel, size, cap, tile),
+        out_shape=(
+            jax.ShapeDtypeStruct((rows, width), jnp.bfloat16),
+            jax.ShapeDtypeStruct(mid_latent.shape, jnp.bfloat16),
+        ),
+        in_specs=[vmem, vmem, hbm, hbm],
+        out_specs=(vmem, vmem),
+        scratch_shapes=[
+            pltpu.VMEM((width, hidden_width), jnp.bfloat16),
+            pltpu.VMEM((hidden_width, width), jnp.bfloat16),
+            pltpu.VMEM((rows, width), jnp.bfloat16),
+            pltpu.VMEM((rows, width), jnp.bfloat16),
+            pltpu.VMEM((rows // groups, width), jnp.float32),
+            pltpu.VMEM((2, rows // groups, tile), jnp.bfloat16),
+            pltpu.VMEM(mid_latent.shape, jnp.float32),
+            pltpu.SemaphoreType.DMA((2,)),
+            pltpu.SemaphoreType.DMA((2,)),
+            pltpu.SemaphoreType.DMA((2,)),
+            pltpu.SemaphoreType.DMA((size,)),
+            pltpu.SemaphoreType.DMA((size,)),
+            pltpu.SemaphoreType.DMA((size,)),
+            pltpu.SemaphoreType.DMA((size,)),
+        ],
+        compiler_params=pltpu.CompilerParams(
+            collective_id=0, has_side_effects=True, vmem_limit_bytes=48 * 1024 * 1024
+        ),
+    )(mid_latent, buffer, weight_in, weight_out)
+
+
+def mixture(mid_tokens, mid_latent, chosen, slot_ids, scales, router, fc_in, fc_out):
     model_width = mid_tokens.shape[1]
     expert_count = router.shape[1]
     capacity = CAP_FACTOR * mid_tokens.shape[0] // expert_count
@@ -80,28 +259,16 @@
     gate_value = jax.nn.sigmoid(picked)
     served = slot_ids < capacity
     position = jnp.where(served, chosen * capacity + slot_ids, slot_total)
-    buffer = (
-        jnp.zeros((slot_total, model_width), jnp.bfloat16).at[position].set(expert_in, mode="drop")
-    )
-    buffer = buffer.reshape(expert_count, capacity, model_width)
-    results = lax.all_to_all(
-        apply_experts(
-            lax.all_to_all(buffer, "exp", split_axis=0, concat_axis=0, tiled=True), fc_in, fc_out
-        ),
-        "exp",
-        split_axis=0,
-        concat_axis=0,
-        tiled=True,
-    )
-    returned = jnp.take(
-        results.reshape(slot_total, model_width), position, axis=0, mode="fill", fill_value=0
-    )
-    return (mid_tokens + gate_value[:, None] * returned.astype(jnp.float32)).astype(jnp.bfloat16)
-
-
-def average_latent(mid_latent):
-    summed = lax.psum(mid_latent.astype(jnp.bfloat16), "mod").astype(jnp.float32)
-    return (summed * 0.5).astype(jnp.bfloat16)
+    places = jnp.arange(slot_total, dtype=jnp.int32)
+    to_slot = (places[:, None] == position[None, :]).astype(jnp.bfloat16)
+    buffer = jnp.dot(to_slot, expert_in, preferred_element_type=jnp.float32).astype(jnp.bfloat16)
+    results, new_bottleneck = exchange_experts(
+        mid_latent.reshape(-1, model_width), buffer, fc_in[0], fc_out[0], expert_count
+    )
+    from_slot = (position[:, None] == places[None, :]).astype(jnp.bfloat16)
+    returned = jnp.dot(from_slot, results, preferred_element_type=jnp.float32)
+    mixed = (mid_tokens + gate_value[:, None] * returned).astype(jnp.bfloat16)
+    return mixed, new_bottleneck.reshape(mid_latent.shape)
 
 
 def on_device(
@@ -122,9 +289,8 @@
     mid_tokens, mid_latent = attend(
         tokens[0], bottleneck, clip_ids[0], clip_start, norm1_gain[0], attn_qkv[0], attn_out[0]
     )
-    new_bottleneck = average_latent(mid_latent)
-    mixed_tokens = mixture(
-        mid_tokens, expert_ids[0], slots[0], norm2_gain[0], router, fc_in, fc_out
+    mixed_tokens, new_bottleneck = mixture(
+        mid_tokens, mid_latent, expert_ids[0], slots[0], norm2_gain[0], router, fc_in, fc_out
     )
     return (mixed_tokens[None], new_bottleneck)
 

time: 222 us -> 150 us (0.68); the launches traced: 219 us -> 150 us
  Pallas kernels: 0 us -> 99.5 us
  blocking collectives: 58.6 us -> 0 us
  matrix products: 89.5 us -> 35.4 us
  waiting for transfers between devices: 34.5 us -> 0 us
  other arithmetic: 13.4 us -> 4.32 us
  starting transfers between devices: 5.99 us -> 0 us
  local copies, waits for them, and re-layouts: 15.7 us -> 9.88 us
    pallas_call x0 -> x1, Pallas kernels: none -> 99.5 us  [exchange_experts(): pl.pallas_call(functools.partial(moe_kernel, size, cap, tile), out_shape=...]
    dot_general x2, matrix products: 57.1 us -> 3.53 us  [the longest x1 2.28 us: mixture(): returned = jnp.dot(from_slot, results, preferred_element_type=jnp.float32)]
    all_to_all x1 -> x0, blocking collectives: 52.4 us -> none  [mixture(): lax.all_to_all(buffer, 'exp', split_axis=0, concat_axis=0, tiled=True)]
    all_to_all x1 -> x0, waiting for transfers between devices: 34.5 us -> none  [mixture(): lax.all_to_all(apply_experts(lax.all_to_all(buffer, 'exp', split_axis=0,...]
    psum x1 -> x0, blocking collectives: 6.14 us -> none  [average_latent(): lax.psum(mid_latent.astype(jnp.bfloat16), 'mod').astype(jnp.float32)]
    all_to_all x1 -> x0, starting transfers between devices: 5.99 us -> none  [mixture(): lax.all_to_all(apply_experts(lax.all_to_all(buffer, 'exp', split_axis=0,...]
    gather x1 -> x0, local copies, waits for them, and re-layouts: 4.74 us -> none  [mixture(): jnp.take(results.reshape(slot_total, model_width), position, axis=0, mode...]
    scatter x1 -> x0, other arithmetic: 4.45 us -> none  [mixture(): jnp.zeros((slot_total, model_width), jnp.bfloat16).at[position]]
  transfers between devices with their start and end apart: 1 -> 0, of which waited for: 1 -> 0; matrix products, arithmetic and copies ran while one was open for 2% -> 0% of each run, Pallas kernels for 0% -> 0%
where the time goes in v1:
time: 150 us
  Pallas kernels  99.5 us (66%)
  matrix products  35.4 us (24%)
  local copies, waits for them, and re-layouts  9.88 us (7%)
  other arithmetic  4.32 us (3%)
    pallas_call x1, Pallas kernels, exchange_experts(): pl.pallas_call(functools.partial(moe_kernel, size, cap, tile), out_shape=...  99.5 us
    sub x1, matrix products, attend(): weights = jnp.exp(scores - row_max)  13.2 us
    dot_general x1, matrix products, attend(): jnp.einsum('hqk,khd->qhd', attn_weights, value_rows, preferred_element_ty...  9.81 us
    dot_general x1, matrix products, attend(): jnp.dot(normed, w_qkv, preferred_element_type=jnp.float32)  7.12 us
    slice x2, local copies, waits for them, and re-layouts, attend(): packed[:, model_width:2 * model_width].reshape(row_count, head_count, HEAD)  4.06 us

profile of v1, /device:TPU:29, one launch (start us, length us, event | category | flops | bytes accessed | tf_op | source)
XLA Modules:
  0.0 149.9 jit_solution(13066406522153010018)
XLA Ops:
  0.6 0.0 copy-start
  0.7 0.9 reshape.96
  1.6 1.5 convert_reduce_fusion
  3.1 1.7 %fusion.13 = f32[528]{0:T(1024)S(1)} fusion(f32[528]{0:T(1024)S(1)} %broadcast_multiply_fusion, bf16[16,1024]{1,0:T(8,128)(2,1)S(1)} %reshape.96, bf16[512,1024]{1,0:T(8,128)(2,1)} %bitcast.40), kind=kLoop, calls=%fused_computation.17 | loop fusion | flops 3784176 | bytes 1085568 | tf_op jit(solution)/shard_map/reduce_sum | solution.py:22
  4.8 7.1 %fusion.8 = bf16[528,3072]{1,0:T(8,128)(2,1)S(1)} fusion(bf16[1,1024,3072]{2,1,0:T(8,128)(2,1)} %param.18, f32[1024]{0:T(1024)S(1)} %bitcast.50, f32[528]{0:T(1024)S(1)} %add_rsqrt_fusion, f32[528]{0:T(1024)S(1)} %broadcast_multiply_fusion, bf16[16,1024]{1,0:T(8,128)(2,1)S(1)} %reshape.96, bf16[512,1024]{1,0:T(8,128)(2,1)S(1)} %bitcast.41), kind=kOutput, calls=%fused_computation.11 | convolution fusion | flops 3327836160 | bytes 10625152 | tf_op jit(solution)/shard_map/dot_general | solution.py:35
  11.9 1.7 %fusion.37 = (bf16[528,1024]{1,0:T(8,128)(2,1)}, bf16[528,1024]{1,0:T(8,128)(2,1)}, bf16[528,1024]{1,0:T(8,128)(2,1)S(1)}) fusion(bf16[528,3072]{1,0:T(8,128)(2,1)S(1)} %fusion.8), kind=kLoop, calls=%fused_computation.59 | loop fusion | bytes 6488064 | tf_op jit(solution)/shard_map/slice | solution.py:37
  13.6 2.4 %copy.19 = bf16[528,1024]{0,1:T(8,128)(2,1)} copy(bf16[528,1024]{1,0:T(8,128)(2,1)} %get-tuple-element.7) | data formatting | bytes 2162688 | tf_op jit(solution)/shard_map/slice | solution.py:36
  16.0 2.4 %copy.20 = bf16[528,1024]{0,1:T(8,128)(2,1)} copy(bf16[528,1024]{1,0:T(8,128)(2,1)} %get-tuple-element.6) | data formatting | bytes 2162688 | tf_op jit(solution)/shard_map/slice | solution.py:37
  18.4 0.3 broadcast_compare_fusion
  18.7 13.2 %fusion.38 = (f32[16,528]{1,0:T(8,128)}, f32[16,528,528]{1,2,0:T(8,128)}) fusion(pred[528,528]{0,1:T(8,128)(4,1)S(1)} %broadcast_compare_fusion, bf16[528,16,64]{0,2,1:T(8,128)(2,1)} %bitcast.43, bf16[528,16,64]{0,2,1:T(8,128)(2,1)} %bitcast.44), kind=kOutput, calls=%fused_computation.60 | convolution fusion | flops 588792320 | bytes 20317440 | tf_op jit(solution)/shard_map/sub | solution.py:47
  31.9 1.4 copy.18
  33.3 9.8 %fusion.21 = bf16[16,64,528]{2,1,0:T(8,128)(2,1)S(1)} fusion(bf16[528,16,64]{0,2,1:T(8,128)(2,1)} %bitcast.45, f32[16,528,528]{1,2,0:T(8,128)} %get-tuple-element.10, f32[16,528]{1,0:T(8,128)S(1)} %copy-done.9), kind=kOutput, calls=%fused_computation.31 | convolution fusion | flops 580411392 | bytes 20038656 | tf_op jit(solution)/shard_map/hqk,khd->qhd/dot_general | solution.py:49
  43.2 1.3 convert_add_fusion
  44.5 0.2 slice_reduce_fusion
  44.7 0.3 multiply_reduce_fusion
  45.1 0.1 copy-done.7
  45.2 0.3 multiply_convert_fusion
  45.5 0.2 copy-done.4
  45.7 0.0 copy-done.5
  45.8 1.2 fusion.20.buf_ref
  47.0 99.5 %shard_map.131 = (bf16[1024,1024]{1,0:T(8,128)(2,1)S(1)}, bf16[16,1024]{1,0:T(8,128)(2,1)S(1)}) custom-call(f32[16,1024]{1,0:T(8,128)S(1)} %slice.24.latent_ref, bf16[1024,1024]{1,0:T(8,128)(2,1)S(1)} %fusion.20.buf_ref, bf16[1024,4096]{1,0:T(8,128)(2,1)} %bitcast.37, bf16[4096,1024]{1,0:T(8,128)(2,1)} %bitcast.38), custom_call_target="tpu_custom_call" | custom-call | tf_op jit(solution)/shard_map/pallas_call | solution.py:218
  146.6 0.4 fusion.27
  147.0 2.3 %fusion.26 = bf16[1,512,1024]{2,1,0:T(8,128)(2,1)} fusion(bf16[1024,1024]{1,0:T(8,128)(2,1)S(1)} %get-tuple-element.4, f32[528,1024]{1,0:T(8,128)S(1)} %convert_add_fusion, s32[512]{0:T(512)S(1)} %add_select_fusion, f32[512]{0:T(512)S(1)} %add_divide_fusion), kind=kOutput, calls=%fused_computation.33 | convolution fusion | flops 1075838976 | bytes 5246976 | tf_op jit(solution)/shard_map/dot_general | solution.py:269
  149.3 0.6 reshape.100
  (28 shorter events, 0.1 us)
Async XLA Ops:
  0.6 42.5 %copy-start = (bf16[1,1024,1024]{2,1,0:T(8,128)(2,1)S(1)}, bf16[1,1024,1024]{2,1,0:T(8,128)(2,1)}, u32[]{:S(2)}) copy-start(bf16[1,1024,1024]{2,1,0:T(8,128)(2,1)} %param.19) | copy-start | bytes 6291460
  0.6 4.1 %copy-start.1 = (bf16[1,512,1024]{2,1,0:T(8,128)(2,1)S(1)}, bf16[1,512,1024]{2,1,0:T(8,128)(2,1)}, u32[]{:S(2)}) copy-start(bf16[1,512,1024]{2,1,0:T(8,128)(2,1)} %param.12) | copy-start | bytes 3145732
  0.7 4.1 %copy-start.6 = (bf16[1,1024]{1,0:T(2,128)(2,1)S(1)}, bf16[1,1024]{1,0:T(2,128)(2,1)}, u32[]{:S(2)}) copy-start(bf16[1,1024]{1,0:T(2,128)(2,1)} %param.17) | copy-start | bytes 6148
  13.6 4.8 %copy-start.8 = (s32[1,512]{1,0:T(1,128)S(1)}, s32[1,512]{1,0:T(1,128)}, u32[]{:S(2)}) copy-start(s32[1,512]{1,0:T(1,128)} %param.14) | copy-start | bytes 6148
  31.9 1.5 copy-start.9
  33.3 9.8 %copy-start.2 = (bf16[1,512,1024]{2,1,0:T(8,128)(2,1)S(1)}, bf16[1,512,1024]{2,1,0:T(8,128)(2,1)}, u32[]{:S(2)}) copy-start(bf16[1,512,1024]{2,1,0:T(8,128)(2,1)} %param.12) | copy-start | bytes 3145732
  44.5 0.7 copy-start.7
  45.0 0.7 copy-start.4
  45.0 0.7 copy-start.5
  47.0 99.5 %copy-start.3 = (bf16[1024,16]{0,1:T(8,128)(2,1)S(1)}, bf16[1024,16]{0,1:T(8,128)(2,1)}, u32[]{:S(2)}) copy-start(bf16[1024,16]{0,1:T(8,128)(2,1)} %param.21) | copy-start | bytes 98308

commit v2 on v1

--- a/solution.py
+++ b/solution.py
@@ -23,6 +23,53 @@
     return centred * lax.rsqrt(spread + EPSILON) * scales.astype(jnp.float32)
 
 
+def attention_kernel(pair, rows_ref, cols_ref, q_ref, k_ref, v_ref, out_ref):
+    allowed = rows_ref[...] == cols_ref[...]
+    lane = lax.broadcasted_iota(jnp.int32, q_ref.shape, 1) // HEAD
+    queries = q_ref[...] * jnp.bfloat16(1.0 / math.sqrt(HEAD))
+    attended = jnp.zeros(out_ref.shape, jnp.float32)
+    for head in range(pair):
+        mine = lane == head
+        scores = lax.dot_general(
+            jnp.where(mine, queries, jnp.zeros_like(queries)),
+            k_ref[...],
+            (((1,), (1,)), ((), ())),
+            preferred_element_type=jnp.float32,
+        )
+        scores = jnp.where(allowed, scores, -jnp.inf)
+        weights = jnp.exp(scores - jnp.max(scores, axis=-1, keepdims=True))
+        total = jnp.sum(weights, axis=-1, keepdims=True)
+        summed = jnp.dot(
+            weights.astype(jnp.bfloat16), v_ref[...], preferred_element_type=jnp.float32
+        )
+        attended = jnp.where(mine, summed / total, attended)
+    out_ref[...] = attended.astype(jnp.bfloat16)
+
+
+def attention(packed, row_clip):
+    rows, width = packed.shape[0], packed.shape[1] // 3
+    pair = 128 // HEAD
+    steps = width // 128
+
+    def part(index):
+        return pl.BlockSpec((rows, 128), lambda step: (0, index * steps + step))
+
+    return pl.pallas_call(
+        functools.partial(attention_kernel, pair),
+        grid=(steps,),
+        out_shape=jax.ShapeDtypeStruct((rows, width), jnp.bfloat16),
+        in_specs=[
+            pl.BlockSpec((rows, 1), lambda step: (0, 0)),
+            pl.BlockSpec((1, rows), lambda step: (0, 0)),
+            part(0),
+            part(1),
+            part(2),
+        ],
+        out_specs=pl.BlockSpec((rows, 128), lambda step: (0, step)),
+        compiler_params=pltpu.CompilerParams(vmem_limit_bytes=32 * 1024 * 1024),
+    )(row_clip[:, None], row_clip[None, :], packed, packed, packed)
+
+
 def attend(token_rows, latent_rows, token_clip, clip_start, scales, w_qkv, w_out):
     n_clips, n_latent, model_width = latent_rows.shape
     n_tokens = token_rows.shape[0]
@@ -30,26 +77,11 @@
         [token_rows, latent_rows.reshape(n_clips * n_latent, model_width)], axis=0
     )
     row_count = all_rows.shape[0]
-    head_count = model_width // HEAD
     normed = layer_norm(all_rows.astype(jnp.float32), scales).astype(jnp.bfloat16)
     packed = jnp.dot(normed, w_qkv, preferred_element_type=jnp.float32).astype(jnp.bfloat16)
-    queries = packed[:, :model_width].reshape(row_count, head_count, HEAD)
-    key_rows = packed[:, model_width : 2 * model_width].reshape(row_count, head_count, HEAD)
-    value_rows = packed[:, 2 * model_width :].reshape(row_count, head_count, HEAD)
     latent_clip = clip_start + jnp.arange(n_clips * n_latent, dtype=jnp.int32) // n_latent
     row_clip = jnp.concatenate([token_clip, latent_clip])
-    allowed = row_clip[:, None] == row_clip[None, :]
-    scores = jnp.einsum("qhd,khd->hqk", queries, key_rows, preferred_element_type=jnp.float32) * (
-        1.0 / math.sqrt(HEAD)
-    )
-    scores = jnp.where(allowed[None, :, :], scores, -jnp.inf)
-    row_max = jnp.max(scores, axis=-1, keepdims=True)
-    weights = jnp.exp(scores - row_max)
-    attn_weights = (weights / jnp.sum(weights, axis=-1, keepdims=True)).astype(jnp.bfloat16)
-    attended = jnp.einsum(
-        "hqk,khd->qhd", attn_weights, value_rows, preferred_element_type=jnp.float32
-    )
-    attended = attended.reshape(row_count, model_width).astype(jnp.bfloat16)
+    attended = attention(packed, row_clip)
     updated = all_rows.astype(jnp.float32) + jnp.dot(
         attended, w_out, preferred_element_type=jnp.float32
     )
@@ -159,7 +191,7 @@
     own.start()
     own.wait()
 
-    groups = 4 if size % 4 == 0 else 1
+    groups = 2 if size % 4 == 0 else 1
     per = size // groups
     rows = per * cap
     tiles = w_in.shape[1] // tile
@@ -211,8 +243,8 @@
     rows, width = buffer.shape
     cap = rows // size
     hidden_width = weight_in.shape[1]
-    tile = 512
-    groups = 4 if size % 4 == 0 else 1
+    tile = 1024
+    groups = 2 if size % 4 == 0 else 1
     vmem = pl.BlockSpec(memory_space=pltpu.VMEM)
     hbm = pl.BlockSpec(memory_space=pl.ANY)
     return pl.pallas_call(

time: 150 us -> 136 us (0.907)
  the two profiles are of different devices: /device:TPU:29 before, /device:TPU:0 now
where the time goes in v2:
time: 136 us; the launch traced here: 135 us
  Pallas kernels  113 us (83%)
  matrix products  12.4 us (9%)
  other arithmetic  7.71 us (6%)
  local copies, waits for them, and re-layouts  1.95 us (1%)
    pallas_call x1, Pallas kernels, exchange_experts(): pl.pallas_call(functools.partial(moe_kernel, size, cap, tile), out_shape=...  98.2 us
    pallas_call x1, Pallas kernels, attention(): pl.pallas_call(functools.partial(attention_kernel, pair), grid=(steps,),...  14.4 us
    dot_general x1, matrix products, attend(): jnp.dot(normed, w_qkv, preferred_element_type=jnp.float32)  7.12 us

profile of v2, /device:TPU:0, one launch (start us, length us, event | category | flops | bytes accessed | tf_op | source)
XLA Modules:
  0.0 135.5 jit_solution(18094258901326215341)
XLA Ops:
  0.6 0.0 copy-start
  0.6 0.0 copy-start.1
  0.7 0.9 add_select_fusion
  1.5 0.8 compare_select_fusion
  2.3 0.7 pad_add_fusion
  3.0 0.7 mul.88
  3.7 0.7 mul.89
  4.4 0.8 reshape.56
  5.2 1.5 %convert_reduce_fusion = f32[528]{0:T(1024)S(1)} fusion(bf16[16,1024]{1,0:T(8,128)(2,1)S(1)} %reshape.56, bf16[512,1024]{1,0:T(8,128)(2,1)} %bitcast.28), kind=kLoop, calls=%fused_computation.5 | loop fusion | flops 2702832 | bytes 1083456 | tf_op jit(solution)/shard_map/reduce_sum | solution.py:20
  6.6 1.7 %fusion.7 = f32[528]{0:T(1024)S(1)} fusion(f32[528]{0:T(1024)S(1)} %broadcast_multiply_fusion, bf16[16,1024]{1,0:T(8,128)(2,1)S(1)} %reshape.56, bf16[512,1024]{1,0:T(8,128)(2,1)} %bitcast.29), kind=kLoop, calls=%fused_computation.8 | loop fusion | flops 3784176 | bytes 1085568 | tf_op jit(solution)/shard_map/reduce_sum | solution.py:22
  8.3 0.1 broadcast_in_dim.36.rows_ref
  8.4 7.1 %fusion.2.q_ref.k_ref.v_ref = bf16[528,3072]{1,0:T(8,128)(2,1)S(1)} fusion(bf16[1,1024,3072]{2,1,0:T(8,128)(2,1)} %param.18, f32[1024]{0:T(1024)S(1)} %bitcast.36, f32[528]{0:T(1024)S(1)} %add_rsqrt_fusion, f32[528]{0:T(1024)S(1)} %broadcast_multiply_fusion, bf16[16,1024]{1,0:T(8,128)(2,1)S(1)} %reshape.56, bf16[512,1024]{1,0:T(8,128)(2,1)S(1)} %bitcast.30), kind=kOutput, calls=%fused_computation.2 | convolution fusion | flops 3327836160 | bytes 10625152 | tf_op jit(solution)/shard_map/dot_general | solution.py:81
  15.6 14.4 %shard_map.131 = bf16[528,1024]{1,0:T(8,128)(2,1)S(1)} custom-call(s32[528,1]{1,0:T(8,128)S(1)} %broadcast_in_dim.36.rows_ref, s32[1,528]{1,0:T(1,128)S(1)} %broadcast_in_dim.15.cols_ref, bf16[528,3072]{1,0:T(8,128)(2,1)S(1)} %fusion.2.q_ref.k_ref.v_ref, bf16[528,3072]{1,0:T(8,128)(2,1)S(1)} %fusion.2.q_ref.k_ref.v_ref, ...), custom_call_target="tpu_custom_call" | custom-call | tf_op jit(solution)/shard_map/pallas_call | solution.py:57
  30.0 1.3 convert_add_fusion
  31.3 0.2 slice_reduce_fusion
  31.5 0.3 multiply_reduce_fusion
  31.9 0.0 copy-start.3
  31.9 0.3 multiply_convert_fusion
  32.3 0.4 copy-done.2
  32.6 0.4 fusion.18
  33.1 1.3 fusion.14.buf_ref
  34.3 98.2 %shard_map.132 = (bf16[1024,1024]{1,0:T(8,128)(2,1)S(1)}, bf16[16,1024]{1,0:T(8,128)(2,1)S(1)}) custom-call(f32[16,1024]{1,0:T(8,128)S(1)} %slice.9.latent_ref, bf16[1024,1024]{1,0:T(8,128)(2,1)S(1)} %fusion.14.buf_ref, bf16[1024,4096]{1,0:T(8,128)(2,1)} %bitcast.26, bf16[4096,1024]{1,0:T(8,128)(2,1)} %bitcast.27), custom_call_target="tpu_custom_call" | custom-call | tf_op jit(solution)/shard_map/pallas_call | solution.py:250
  132.6 2.3 %fusion.17 = bf16[1,512,1024]{2,1,0:T(8,128)(2,1)} fusion(bf16[1024,1024]{1,0:T(8,128)(2,1)S(1)} %get-tuple-element.4, f32[528,1024]{1,0:T(8,128)S(1)} %convert_add_fusion, s32[512]{0:T(512)S(1)} %add_select_fusion, f32[512]{0:T(512)S(1)} %add_divide_fusion), kind=kOutput, calls=%fused_computation.22 | convolution fusion | flops 1075838976 | bytes 5246976 | tf_op jit(solution)/shard_map/dot_general | solution.py:301
  134.8 0.6 reshape.57
  (12 shorter events, 0.1 us)
Async XLA Ops:
  0.6 29.4 %copy-start = (bf16[1,1024,1024]{2,1,0:T(8,128)(2,1)S(1)}, bf16[1,1024,1024]{2,1,0:T(8,128)(2,1)}, u32[]{:S(2)}) copy-start(bf16[1,1024,1024]{2,1,0:T(8,128)(2,1)} %param.19) | copy-start | bytes 6291460
  0.6 7.8 %copy-start.1 = (bf16[1,512,1024]{2,1,0:T(8,128)(2,1)S(1)}, bf16[1,512,1024]{2,1,0:T(8,128)(2,1)}, u32[]{:S(2)}) copy-start(bf16[1,512,1024]{2,1,0:T(8,128)(2,1)} %param.12) | copy-start | bytes 3145732
  31.9 0.8 copy-start.2
  31.9 0.8 copy-start.3
